TPU v7x, 32 devices: a whole 2x2x4 slice. The times are simulated.
32 devices in a mesh: fsdp: 16 (over z, y, x), rep: 2 (over core).
Axes of the slice: x: 2, y: 2, z: 4, core: 2. Of those that a mesh axis runs over, the one named last changes fastest.
Arguments:
- params: float32 [1536, 3584], P(('fsdp', 'rep')), may hold values from -6 to 6
- grads: bfloat16 [1536, 3584], P(('fsdp', 'rep')), may hold values from -6 to 6
- moments: bfloat16 [3, 1536, 3584], P(None, ('fsdp', 'rep')), may hold values from -6 to 6
- row_acc: float32 [1536], P(('fsdp', 'rep')), may hold values from 0.05 to 1
- lengths: int32 [32], replicated, may hold values from 1 to 384, 1536 in all
- tensor_order: int32 [32], replicated, may hold values from 0 to 31, each once
- col_acc: float32 [32, 3584], P('fsdp'), may hold values from 0.05 to 1
- hidden_state: float32 [32, 512], P('fsdp'), may hold values from -1 to 1
- cell_state: float32 [32, 512], P('fsdp'), may hold values from -4 to 4
- lstm_in: bfloat16 [10, 2048], replicated, may hold values from -2 to 2
- lstm_rec: bfloat16 [512, 2048], replicated, may hold values from -0.25 to 0.25
- lstm_bias: float32 [2048], replicated, may hold values from -3 to 3
- hyper_first: bfloat16 [512, 256], replicated, may hold values from -0.25 to 0.25
- hyper_rest: bfloat16 [512, 128], replicated, may hold values from -0.25 to 0.25
Outputs:
- update: float32 [1536, 3584], P(('fsdp', 'rep'))
- row_new: float32 [1536], P(('fsdp', 'rep'))
- col_new: float32 [32, 3584], P('fsdp')
- hidden_new: float32 [32, 512], P('fsdp')
- cell_new: float32 [32, 512], P('fsdp')
Inputs may be any that keep to these rules, and one draw needn't show every extreme that they name: `lengths`: they sum to 1536; the largest is 384. `tensor_order`: owner slot i belongs to fsdp index i // 2; each tensor appears once.
All inputs are finite; a program needn't handle non-finite values.
Results may differ from a plain program's by a relative error of at most 0.019.
Values may be sent and summed in bfloat16 or wider, within the bound.
A program may use at most 64 MiB of HBM per device.

v0:
```python
import math

import jax
import jax.numpy as jnp
from jax import lax
from jax.sharding import PartitionSpec as P

EPSILON = 1e-06
DECAY_RATE = 0.9


def owner_step(
    col_sums,
    tensor_stats,
    row_lengths,
    col_acc,
    hidden_state,
    cell_state,
    lstm_in,
    lstm_rec,
    lstm_bias,
    hyper_first,
    hyper_rest,
):
    col_width = col_acc.shape[1]
    col_new = DECAY_RATE * col_acc + (1.0 - DECAY_RATE) * col_sums / row_lengths[:, None]
    tensor_means = tensor_stats / (row_lengths * col_width)[:, None]
    log_means = jnp.log(tensor_means[:, :5] + EPSILON)
    corr_first = tensor_means[:, 5] / jnp.sqrt(tensor_means[:, 0] * tensor_means[:, 1] + EPSILON)
    corr_second = tensor_means[:, 6] / jnp.sqrt(tensor_means[:, 0] * tensor_means[:, 3] + EPSILON)
    corr_third = tensor_means[:, 7] / jnp.sqrt(tensor_means[:, 1] * tensor_means[:, 3] + EPSILON)
    col_mean = jnp.mean(col_new, axis=1)
    col_square = jnp.mean(col_new * col_new, axis=1)
    spread = jnp.log(col_square / (col_mean * col_mean))
    extra = jnp.stack(
        [corr_first, corr_second, corr_third, jnp.log(col_mean + EPSILON), spread], axis=1
    )
    features = jnp.concatenate([log_means, extra], axis=1).astype(jnp.bfloat16)
    gate_sum = jnp.dot(features, lstm_in, preferred_element_type=jnp.float32)
    gate_sum = (
        gate_sum
        + jnp.dot(hidden_state.astype(jnp.bfloat16), lstm_rec, preferred_element_type=jnp.float32)
        + lstm_bias
    )
    hid_width = hidden_state.shape[1]
    gate_in = gate_sum[:, :hid_width]
    gate_forget = gate_sum[:, hid_width : 2 * hid_width]
    gate_cand = gate_sum[:, 2 * hid_width : 3 * hid_width]
    gate_out = gate_sum[:, 3 * hid_width :]
    cell_new = jax.nn.sigmoid(gate_forget) * cell_state + jax.nn.sigmoid(gate_in) * jnp.tanh(
        gate_cand
    )
    hidden_new = jax.nn.sigmoid(gate_out) * jnp.tanh(cell_new)
    hidden_bf = hidden_new.astype(jnp.bfloat16)
    gen_first = jnp.dot(hidden_bf, hyper_first, preferred_element_type=jnp.float32).astype(
        jnp.bfloat16
    )
    gen_rest = jnp.dot(hidden_bf, hyper_rest, preferred_element_type=jnp.float32).astype(
        jnp.bfloat16
    )
    tensor_scales = jnp.stack(
        [
            jnp.sqrt(tensor_means[:, 0] + EPSILON),
            jnp.sqrt(tensor_means[:, 1] + EPSILON),
            jnp.sqrt(tensor_means[:, 4] + EPSILON),
            col_mean,
        ],
        axis=1,
    )
    return (col_new, hidden_new, cell_new, gen_first, gen_rest, tensor_scales)


def param_block(
    param_rows, grad_rows, moment_rows, row_var, col_rows, first_rows, rest_rows, scale_rows
):
    block_rows = param_rows.shape[0]
    grad_f = grad_rows.astype(jnp.float32)
    mom_f = moment_rows.astype(jnp.float32)
    v_factored = row_var[:, None] * col_rows / scale_rows[:, 3:4]
    inv_rms = lax.rsqrt(v_factored + EPSILON)
    grad_norm = grad_f * inv_rms
    mom_norm = mom_f[0] * inv_rms
    inputs = jnp.stack(
        [
            grad_norm,
            mom_norm,
            mom_f[1] * inv_rms,
            mom_f[2] * inv_rms,
            grad_f / scale_rows[:, 0:1],
            mom_f[0] / scale_rows[:, 1:2],
            param_rows / scale_rows[:, 2:3],
            grad_norm * mom_norm,
        ],
        axis=1,
    ).astype(jnp.bfloat16)
    hm_width = rest_rows.shape[1] // 4
    w_first = first_rows.reshape(block_rows, 8, hm_width)
    bias_first = rest_rows[:, :hm_width].astype(jnp.float32)
    w_second = rest_rows[:, hm_width:].reshape(block_rows, hm_width, 3)
    hidden_units = (
        jnp.einsum("bfc,bfh->bhc", inputs, w_first, preferred_element_type=jnp.float32)
        + bias_first[:, :, None]
    )
    hidden_units = jax.nn.relu(hidden_units).astype(jnp.bfloat16)
    mlp_out = jnp.einsum("bhc,bho->boc", hidden_units, w_second, preferred_element_type=jnp.float32)
    return mlp_out[:, 0] * jnp.exp(jnp.tanh(mlp_out[:, 1])) * jax.nn.sigmoid(mlp_out[:, 2])


def on_device(
    params,
    grads,
    moments,
    row_acc,
    lengths,
    tensor_order,
    col_acc,
    hidden_state,
    cell_state,
    lstm_in,
    lstm_rec,
    lstm_bias,
    hyper_first,
    hyper_rest,
):
    row_count = params.shape[0]
    tensor_count = lengths.shape[0]
    own_count = col_acc.shape[0]
    first_row = (lax.axis_index("fsdp") * lax.axis_size("rep") + lax.axis_index("rep")) * row_count
    tensor_ends = jnp.cumsum(lengths)
    global_rows = first_row + lax.iota(jnp.int32, row_count)
    seg_ids = jnp.sum((global_rows[:, None] >= tensor_ends[None, :]).astype(jnp.int32), axis=1)
    row_pick = (seg_ids[:, None] == tensor_order[None, :]).astype(jnp.float32)
    slot_match = tensor_order[:, None] == lax.iota(jnp.int32, tensor_count)[None, :]
    row_lengths = jnp.sum(jnp.where(slot_match, lengths[None, :], 0), axis=1).astype(jnp.float32)
    grad_f = grads.astype(jnp.float32)
    grad_sq = grad_f * grad_f
    row_new = DECAY_RATE * row_acc + (1.0 - DECAY_RATE) * jnp.mean(grad_sq, axis=1)
    mom_zero = moments[0].astype(jnp.float32)
    mom_one = moments[1].astype(jnp.float32)
    mom_two = moments[2].astype(jnp.float32)
    per_row = jnp.stack(
        [
            jnp.sum(grad_sq, axis=1),
            jnp.sum(mom_zero * mom_zero, axis=1),
            jnp.sum(mom_one * mom_one, axis=1),
            jnp.sum(mom_two * mom_two, axis=1),
            jnp.sum(params * params, axis=1),
            jnp.sum(grad_f * mom_zero, axis=1),
            jnp.sum(grad_f * mom_two, axis=1),
            jnp.sum(mom_zero * mom_two, axis=1),
        ],
        axis=1,
    )
    slot_stats = jnp.einsum("ri,rk->ik", row_pick, per_row, precision=lax.Precision.HIGHEST)
    slot_cols = jnp.einsum("ri,rc->ic", row_pick, grad_sq, precision=lax.Precision.HIGHEST)
    mine_start = lax.axis_index("fsdp") * own_count
    col_total, stats_total = lax.psum((slot_cols, slot_stats), ("fsdp", "rep"))
    col_prev, hidden_all, cell_all = (
        lax.all_gather(col_acc, "fsdp", axis=0, tiled=True),
        lax.all_gather(hidden_state, "fsdp", axis=0, tiled=True),
        lax.all_gather(cell_state, "fsdp", axis=0, tiled=True),
    )
    col_all, hidden_every, cell_every, first_all, rest_all, scale_all = owner_step(
        col_total,
        stats_total,
        row_lengths,
        col_prev,
        hidden_all,
        cell_all,
        lstm_in,
        lstm_rec,
        lstm_bias,
        hyper_first,
        hyper_rest,
    )
    col_new = lax.dynamic_slice_in_dim(col_all, mine_start, own_count, 0)
    hidden_new = lax.dynamic_slice_in_dim(hidden_every, mine_start, own_count, 0)
    cell_new = lax.dynamic_slice_in_dim(cell_every, mine_start, own_count, 0)
    col_rows = jnp.dot(row_pick, col_all, precision=lax.Precision.HIGHEST)
    scale_rows = jnp.dot(row_pick, scale_all, precision=lax.Precision.HIGHEST)
    pick_bf = row_pick.astype(jnp.bfloat16)
    first_rows = jnp.dot(pick_bf, first_all, preferred_element_type=jnp.float32).astype(
        jnp.bfloat16
    )
    rest_rows = jnp.dot(pick_bf, rest_all, preferred_element_type=jnp.float32).astype(jnp.bfloat16)
    block_rows = math.gcd(row_count, 16)
    block_count = row_count // block_rows

    def one_block(index):
        start = index * block_rows
        return param_block(
            lax.dynamic_slice_in_dim(params, start, block_rows, 0),
            lax.dynamic_slice_in_dim(grads, start, block_rows, 0),
            lax.dynamic_slice_in_dim(moments, start, block_rows, 1),
            lax.dynamic_slice_in_dim(row_new, start, block_rows, 0),
            lax.dynamic_slice_in_dim(col_rows, start, block_rows, 0),
            lax.dynamic_slice_in_dim(first_rows, start, block_rows, 0),
            lax.dynamic_slice_in_dim(rest_rows, start, block_rows, 0),
            lax.dynamic_slice_in_dim(scale_rows, start, block_rows, 0),
        )

    update = lax.map(one_block, lax.iota(jnp.int32, block_count)).reshape(params.shape)
    return (update, row_new, col_new, hidden_new, cell_new)


def solution(mesh):
    placed = (
        P(("fsdp", "rep"), None),
        P(("fsdp", "rep"), None),
        P(None, ("fsdp", "rep"), None),
        P(("fsdp", "rep")),
        P(),
        P(),
        P("fsdp", None),
        P("fsdp", None),
        P("fsdp", None),
        P(),
        P(),
        P(),
        P(),
        P(),
    )
    return jax.shard_map(
        on_device,
        mesh=mesh,
        in_specs=placed,
        out_specs=(
            P(("fsdp", "rep"), None),
            P(("fsdp", "rep")),
            P("fsdp", None),
            P("fsdp", None),
            P("fsdp", None),
        ),
        check_vma=False,
    )
```

profile of v0, /device:TPU:0, one launch (start us, length us, event | category | flops | bytes accessed | tf_op | source)
XLA Modules:
  0.0 245.1 jit_solution(586881530292995540)
XLA Ops:
  7.3 0.9 copy.76
  8.4 2.3 fusion.25
  10.7 0.9 select_reduce_fusion
  11.6 1.2 multiply_reduce_fusion.1
  12.7 1.7 fusion.30
  14.4 1.2 multiply_reduce_fusion
  16.5 42.0 %psum.14 = f32[32,8]{0,1:T(8,128)S(1)} all-reduce(f32[32,8]{0,1:T(8,128)S(1)} %fusion.50), channel_id=1, replica_groups=mesh['fsdp'=16,'rep'=2] {'fsdp','rep'}, use_global_device_ids=true, to_apply=%region_12.13 | all-reduce | flops 256 | bytes 2048 | tf_op jit(solution)/shard_map/psum | solution.py:157
  58.5 0.6 log_convert_fusion
  59.1 39.8 %all-gather.1 = bf16[16,2,512]{2,1,0:T(2,128)(2,1)S(1)} all-gather(bf16[1,2,512]{2,1,0:T(2,128)(2,1)S(1)} %bitcast_convert_fusion), channel_id=1, replica_groups=mesh['fsdp'=16,'rep'=2] {'fsdp'}, dimensions={0}, use_global_device_ids=true | all-gather | bytes 34816 | tf_op jit(solution)/shard_map/all_gather | solution.py:160
  98.9 38.4 %all-gather = f32[16,2,3584]{2,1,0:T(2,128)S(1)} all-gather(f32[1,2,3584]{2,1,0:T(2,128)S(1)} %bitcast.121), channel_id=1, replica_groups=mesh['fsdp'=16,'rep'=2] {'fsdp'}, dimensions={0}, use_global_device_ids=true | all-gather | bytes 487424 | tf_op jit(solution)/shard_map/all_gather | solution.py:159
  138.1 37.8 %all-gather.2 = f32[16,2,512]{2,1,0:T(2,128)S(1)} all-gather(f32[1,2,512]{2,1,0:T(2,128)S(1)} %bitcast.122), channel_id=1, replica_groups=mesh['fsdp'=16,'rep'=2] {'fsdp'}, dimensions={0}, use_global_device_ids=true | all-gather | bytes 69632 | tf_op jit(solution)/shard_map/all_gather | solution.py:161
  176.9 1.3 multiply_reduce_fusion.2
  178.2 2.0 fusion.47
  180.2 0.6 constant_dynamic-slice_fusion.4
  180.8 0.7 concatenate.4
  181.9 0.6 constant_dynamic-slice_fusion.2
  182.7 0.9 convolution_convert_fusion
  183.8 54.4 %while.10 = (s32[]{:T(128)}, f32[3,16,3584]{2,1,0:T(8,128)}, s32[3]{0:T(128)S(1)}, bf16[48,128]{1,0:T(8,128)(2,1)S(1)}, bf16[48,256]{1,0:T(8,128)(2,1)}, /*index...) while((s32[]{:T(128)}, f32[3,16,3584]{2,1,0:T(8,128)}, ...), condition=%wide.region_16.17_spmd, body=%wide.region_15.16_spmd.sunk | while | flops 47481352 | bytes 11314883 | solution.py:202
  183.8 0.6 dynamic_slice.75
  185.1 0.7 dynamic_slice.76
  186.0 0.7 constant_dynamic-slice_fusion.7
  187.0 1.0 dynamic-slice_convert_fusion.4
  188.4 1.3 fusion.104
  190.6 0.9 copy.132
  191.5 0.9 copy.133
  192.4 5.5 %stack.83 = bf16[16,8,3584]{2,1,0:T(8,128)(2,1)} concatenate(bf16[16,1,3584]{2,1,0:T(2,128)(2,1)S(1)} %copy.127, bf16[16,1,3584]{2,1,0:T(2,128)(2,1)S(1)} %copy.128, bf16[16,1,3584]{2,1,0:T(2,128)(2,1)S(1)} %copy.129, bf16[16,1,3584]{2,1,0:T(2,128)(2,1)S(1)} %copy.130, bf16[16,1,3584]{2,1,0:T(2,128)(2,1)S(1)} %copy.131, bf16[16,1,3584]{2,1,0:T(2,128)(2,1)S(1)} %fusion.105, ...), dimensions={1} | concatenate | bytes 1835008 | tf_op jit(solution)/shard_map/while/body/eval_jaxpr/stack | solution.py:83
  197.9 2.8 %fusion.106 = f32[16,3,3584]{2,1,0:T(4,128)S(1)} fusion(bf16[16,32,3]{1,2,0:T(4,128)(2,1)S(1)} %copy.126, bf16[16,8,32]{2,1,0:T(8,128)(2,1)S(1)} %reshape.216, bf16[16,8,3584]{2,1,0:T(8,128)(2,1)} %stack.83, f32[16,32]{1,0:T(8,128)S(1)} %dynamic-slice_convert_fusion.5), kind=kOutput, calls=%fused_computation.1.clone.1 | convolution fusion | flops 45875200 | bytes 1618944 | tf_op jit(solution)/shard_map/while/body/eval_jaxpr/bhc,bho->boc/dot_general | solution.py:105
  201.2 0.8 fusion.108
  202.0 0.6 dynamic_slice.75
  203.2 0.7 dynamic_slice.76
  204.1 0.7 constant_dynamic-slice_fusion.7
  205.2 1.0 dynamic-slice_convert_fusion.4
  206.5 1.3 fusion.104
  208.8 0.9 copy.132
  209.7 0.9 copy.133
  210.5 5.5 %stack.83 = bf16[16,8,3584]{2,1,0:T(8,128)(2,1)} concatenate(bf16[16,1,3584]{2,1,0:T(2,128)(2,1)S(1)} %copy.127, bf16[16,1,3584]{2,1,0:T(2,128)(2,1)S(1)} %copy.128, bf16[16,1,3584]{2,1,0:T(2,128)(2,1)S(1)} %copy.129, bf16[16,1,3584]{2,1,0:T(2,128)(2,1)S(1)} %copy.130, bf16[16,1,3584]{2,1,0:T(2,128)(2,1)S(1)} %copy.131, bf16[16,1,3584]{2,1,0:T(2,128)(2,1)S(1)} %fusion.105, ...), dimensions={1} | concatenate | bytes 1835008 | tf_op jit(solution)/shard_map/while/body/eval_jaxpr/stack | solution.py:83
  216.0 2.8 %fusion.106 = f32[16,3,3584]{2,1,0:T(4,128)S(1)} fusion(bf16[16,32,3]{1,2,0:T(4,128)(2,1)S(1)} %copy.126, bf16[16,8,32]{2,1,0:T(8,128)(2,1)S(1)} %reshape.216, bf16[16,8,3584]{2,1,0:T(8,128)(2,1)} %stack.83, f32[16,32]{1,0:T(8,128)S(1)} %dynamic-slice_convert_fusion.5), kind=kOutput, calls=%fused_computation.1.clone.1 | convolution fusion | flops 45875200 | bytes 1618944 | tf_op jit(solution)/shard_map/while/body/eval_jaxpr/bhc,bho->boc/dot_general | solution.py:105
  219.3 0.8 fusion.108
  220.1 0.6 dynamic_slice.75
  221.4 0.7 dynamic_slice.76
  222.3 0.7 constant_dynamic-slice_fusion.7
  223.3 1.0 dynamic-slice_convert_fusion.4
  224.7 1.3 fusion.104
  226.9 0.9 copy.132
  227.8 0.9 copy.133
  228.7 5.5 %stack.83 = bf16[16,8,3584]{2,1,0:T(8,128)(2,1)} concatenate(bf16[16,1,3584]{2,1,0:T(2,128)(2,1)S(1)} %copy.127, bf16[16,1,3584]{2,1,0:T(2,128)(2,1)S(1)} %copy.128, bf16[16,1,3584]{2,1,0:T(2,128)(2,1)S(1)} %copy.129, bf16[16,1,3584]{2,1,0:T(2,128)(2,1)S(1)} %copy.130, bf16[16,1,3584]{2,1,0:T(2,128)(2,1)S(1)} %copy.131, bf16[16,1,3584]{2,1,0:T(2,128)(2,1)S(1)} %fusion.105, ...), dimensions={1} | concatenate | bytes 1835008 | tf_op jit(solution)/shard_map/while/body/eval_jaxpr/stack | solution.py:83
  234.2 2.8 %fusion.106 = f32[16,3,3584]{2,1,0:T(4,128)S(1)} fusion(bf16[16,32,3]{1,2,0:T(4,128)(2,1)S(1)} %copy.126, bf16[16,8,32]{2,1,0:T(8,128)(2,1)S(1)} %reshape.216, bf16[16,8,3584]{2,1,0:T(8,128)(2,1)} %stack.83, f32[16,32]{1,0:T(8,128)S(1)} %dynamic-slice_convert_fusion.5), kind=kOutput, calls=%fused_computation.1.clone.1 | convolution fusion | flops 45875200 | bytes 1618944 | tf_op jit(solution)/shard_map/while/body/eval_jaxpr/bhc,bho->boc/dot_general | solution.py:105
  237.4 0.8 fusion.108
  (100 shorter events, 10.0 us)
Async XLA Ops:
  7.2 130.4 %copy-start = (bf16[512,2048]{1,0:T(8,128)(2,1)S(1)}, bf16[512,2048]{1,0:T(8,128)(2,1)}, u32[]{:S(2)}) copy-start(bf16[512,2048]{1,0:T(8,128)(2,1)} %param.26) | copy-start | bytes 6291460
  7.2 9.1 %copy-start.6 = (s32[32]{0:T(128)S(1)}, s32[32]{0:T(128)}, u32[]{:S(2)}) copy-start(s32[32]{0:T(128)} %param.21) | copy-start | bytes 388
  7.2 8.5 %copy-start.10 = (f32[2,512]{1,0:T(2,128)S(1)}, f32[2,512]{1,0:T(2,128)}, u32[]{:S(2)}) copy-start(f32[2,512]{1,0:T(2,128)} %param.23) | copy-start | bytes 12292
  7.2 8.5 %copy-start.11 = (f32[48]{0:T(128)S(1)}, f32[48]{0:T(128)}, u32[]{:S(2)}) copy-start(f32[48]{0:T(128)} %param.19) | copy-start | bytes 580
  7.2 91.7 %copy-start.4 = (f32[2,3584]{1,0:T(2,128)S(1)}, f32[2,3584]{1,0:T(2,128)}, u32[]{:S(2)}) copy-start(f32[2,3584]{1,0:T(2,128)} %param.22) | copy-start | bytes 86020
  7.2 169.6 %all-reduce.2.cloned.1.call-start = ((), (), s32[]{:S(2)}) async-start(), calls=%async_computation | async-start | bytes 917504 | tf_op jit(solution)/shard_map/psum | solution.py:157
  8.4 7.9 %copy-start.7 = (s32[48]{0:T(128)}, s32[48]{0:T(128)S(1)}, u32[]{:S(2)}) copy-start(s32[48]{0:T(128)S(1)} %convert_reduce_fusion) | copy-start | bytes 580
  15.7 122.4 %copy-start.9 = (f32[2,512]{1,0:T(2,128)S(1)}, f32[2,512]{1,0:T(2,128)}, u32[]{:S(2)}) copy-start(f32[2,512]{1,0:T(2,128)} %param.24) | copy-start | bytes 12292
  138.0 43.5 %copy-start.3 = (bf16[10,2048]{1,0:T(8,128)(2,1)S(1)}, bf16[10,2048]{1,0:T(8,128)(2,1)}, u32[]{:S(2)}) copy-start(bf16[10,2048]{1,0:T(8,128)(2,1)} %param.25) | copy-start | bytes 122884
  138.0 43.5 %copy-start.5 = (f32[2048]{0:T(1024)S(1)}, f32[2048]{0:T(1024)}, u32[]{:S(2)}) copy-start(f32[2048]{0:T(1024)} %param.27) | copy-start | bytes 24580
  176.5 6.0 %copy-start.2 = (bf16[512,128]{1,0:T(8,128)(2,1)S(1)}, bf16[512,128]{1,0:T(8,128)(2,1)}, u32[]{:S(2)}) copy-start(bf16[512,128]{1,0:T(8,128)(2,1)} %param.29) | copy-start | bytes 393220
  176.8 5.7 %copy-start.8 = (s32[48]{0:T(128)S(1)}, s32[48]{0:T(128)}, u32[]{:S(2)}) copy-start(s32[48]{0:T(128)} %copy-done.7) | copy-start | bytes 580
  176.8 5.9 %copy-start.1 = (bf16[512,256]{1,0:T(8,128)(2,1)S(1)}, bf16[512,256]{1,0:T(8,128)(2,1)}, u32[]{:S(2)}) copy-start(bf16[512,256]{1,0:T(8,128)(2,1)} %param.28) | copy-start | bytes 786436
Sparse Core Ops, SparseCore 0:
  13.3 130.1 all-reduce.1
where the time goes:
time: 247 us; the launch traced here: 245 us
  blocking collectives  158 us (64%)
  local copies, waits for them, and re-layouts  36.7 us (15%)
  other arithmetic  19 us (8%)
  matrix products  14.8 us (6%)
  between operations  14.3 us (6%)
    psum x1, blocking collectives, on_device(): col_total, stats_total = lax.psum((slot_cols, slot_stats), ('fsdp', 'rep'))  42 us
    all_gather x1, blocking collectives, on_device(): lax.all_gather(hidden_state, 'fsdp', axis=0, tiled=True)  39.8 us
    all_gather x1, blocking collectives, on_device(): lax.all_gather(col_acc, 'fsdp', axis=0, tiled=True)  38.4 us
    all_gather x1, blocking collectives, on_device(): lax.all_gather(cell_state, 'fsdp', axis=0, tiled=True)  37.8 us
    another operation x24, local copies, waits for them, and re-layouts, param_block(): jnp.stack([grad_norm, mom_norm, mom_f[1] * inv_rms, mom_f[2] * inv_rms, g...  24.4 us
    dot_general x3, matrix products, param_block(): jnp.einsum('bhc,bho->boc', hidden_units, w_second, preferred_element_type...  8.4 us
  transfers between devices with their start and end apart: 1, of which 0 were waited for; matrix products, arithmetic and copies ran while one was open for 3% of the time, Pallas kernels for 0%

commit v1 on v0

v1 whole, which is shorter than its diff:
```python
import functools
import math

import jax
import jax.numpy as jnp
from jax import lax
from jax.experimental import pallas as pl
from jax.experimental.pallas import tpu as pltpu
from jax.sharding import PartitionSpec as P

EPSILON = 1e-06
DECAY_RATE = 0.9
LANES = 128
GROUP = 16
STATS = 8
F32 = jnp.float32
BF16 = jnp.bfloat16


def iota(shape, axis):
    return lax.broadcasted_iota(jnp.int32, shape, axis)


def to_column(row):
    size = row.shape[1]
    square = jnp.broadcast_to(row, (size, size))
    return jnp.sum(jnp.where(iota((size, size), 0) == iota((size, size), 1), square, 0.0), 1, keepdims=True)


def to_row(column):
    size = column.shape[0]
    square = jnp.broadcast_to(column, (size, size))
    return jnp.sum(jnp.where(iota((size, size), 0) == iota((size, size), 1), square, 0.0), 0, keepdims=True)


def take_rows(table, first, out):
    for j in range(out.shape[0]):
        mine = iota(table.shape, 0) == first + j
        out[j : j + 1, :] = jnp.sum(jnp.where(mine, table, 0.0), 0, keepdims=True)


def slot_columns(lengths, order):
    count = lengths.shape[1]
    order_col = to_column(order)
    tensor = iota((count, count), 1).astype(F32)
    spread = jnp.broadcast_to(lengths, (count, count))
    start = jnp.sum(jnp.where(tensor < order_col, spread, 0.0), 1, keepdims=True)
    size = jnp.sum(jnp.where(tensor == order_col, spread, 0.0), 1, keepdims=True)
    return start, size


def share_kernel(
    fsdp,
    rep,
    params_ref,
    grads_ref,
    moments_ref,
    lengths_ref,
    order_ref,
    col_acc_ref,
    hidden_ref,
    cell_ref,
    cols_out,
    hidden_out,
    cell_out,
    rows_out,
    part,
    held,
    total,
    cols,
    acc_parts,
    acc_all,
    hidden_parts,
    cell_parts,
    sems,
    send_sem,
    acc_sem,
):
    count = fsdp * rep
    my_f = lax.axis_index("fsdp")
    my_r = lax.axis_index("rep")
    me = my_f * rep + my_r
    row_count, width = params_ref.shape
    slots = lengths_ref.shape[1]
    own = slots // fsdp
    tiles = width // LANES
    all_tiles = tiles + 1
    barrier = pltpu.get_barrier_semaphore()

    def hello(k, _):
        to = lax.rem(me + k, count)
        pl.semaphore_signal(
            barrier,
            inc=1,
            device_id=(to // rep, lax.rem(to, rep)),
            device_id_type=pl.DeviceIdType.MESH,
        )
        return 0

    lax.fori_loop(1, count, hello, 0)

    start, size = slot_columns(lengths_ref[...].astype(F32), order_ref[...].astype(F32))
    row_ids = (me * row_count + iota((slots, row_count), 1)).astype(F32)
    pick = jnp.where((row_ids >= start) & (row_ids < start + size), 1.0, 0.0)

    step = LANES * math.gcd(tiles, 4)
    lane = iota((GROUP, LANES), 1)
    for first in range(0, row_count, GROUP):
        rows = pl.ds(first, GROUP)

        def chunk(k, sums):
            at = pl.ds(pl.multiple_of(k * step, LANES), step)
            g = grads_ref[rows, at].astype(F32)
            m0 = moments_ref[0, rows, at].astype(F32)
            m1 = moments_ref[1, rows, at].astype(F32)
            m2 = moments_ref[2, rows, at].astype(F32)
            p = params_ref[rows, at]
            pairs = ((g, g), (m0, m0), (m1, m1), (m2, m2), (p, p), (g, m0), (g, m2), (m0, m2))
            new = []
            for s, (a, b) in zip(sums, pairs):
                prod = a * b
                for j in range(0, step, LANES):
                    s = s + prod[:, j : j + LANES]
                new.append(s)
            return tuple(new)

        zero = jnp.zeros((GROUP, LANES), F32)
        sums = lax.fori_loop(0, width // step, chunk, (zero,) * STATS)
        row_stats = zero
        for k, s in enumerate(sums):
            row_stats = jnp.where(lax.rem(lane, STATS) == k, jnp.sum(s, 1, keepdims=True), row_stats)
        rows_out[rows, :] = row_stats

    slot_stats = jnp.dot(
        pick, rows_out[...], precision=lax.Precision.HIGHEST, preferred_element_type=F32
    )
    wide_lane = iota((slots, LANES), 1)
    high = slot_stats.astype(BF16).astype(F32)
    part[:, width:] = jnp.where(wide_lane < STATS, high, slot_stats - high).astype(BF16)
    pick_bf = pick.astype(BF16)
    for first in range(0, width, step):
        g = grads_ref[:, first : first + step].astype(F32)
        part[:, first : first + step] = jnp.dot(
            pick_bf, (g * g).astype(BF16), preferred_element_type=F32
        ).astype(BF16)

    pl.semaphore_wait(barrier, count - 1)

    def await_bytes(ref, sem):
        pltpu.make_async_copy(ref, ref, sem).wait()

    def copy(src, dst, which, to_f, to_r, sending=None):
        return pltpu.make_async_remote_copy(
            src_ref=src,
            dst_ref=dst,
            send_sem=send_sem.at[which] if sending is None else sending,
            recv_sem=sems.at[which],
            device_id=(to_f, to_r),
            device_id_type=pl.DeviceIdType.MESH,
        )

    my_tile = pl.ds(pl.multiple_of(jnp.minimum(me, all_tiles - 1) * LANES, LANES), LANES)

    def part_copy(tile):
        return copy(
            part.at[:, pl.ds(tile * LANES, LANES)], held.at[me], 0, tile // rep, tile % rep
        )

    for tile in range(all_tiles):
        pl.when(me != tile)(lambda tile=tile: part_copy(tile).start())

    def acc_copy(q):
        tile = q * rep + my_r
        at = pl.ds(pl.multiple_of(tile * LANES, LANES), LANES)
        return copy(col_acc_ref.at[:, at], acc_parts.at[my_f], 1, q, my_r, acc_sem.at[q])

    acc_steps = -(-tiles // rep)
    for q in range(acc_steps):
        pl.when((q != my_f) & (q * rep + my_r < tiles))(lambda q=q: acc_copy(q).start())

    def state_copies(k):
        to = lax.rem(my_f + k, fsdp)
        return (
            copy(hidden_ref, hidden_parts.at[my_f], 2, to, my_r),
            copy(cell_ref, cell_parts.at[my_f], 3, to, my_r),
        )

    def send_states(k, _):
        for c in state_copies(k):
            c.start()
        return 0

    lax.fori_loop(1, fsdp, send_states, 0)
    hidden_parts[my_f] = hidden_ref[...]
    cell_parts[my_f] = cell_ref[...]

    def tile_sum():
        held[me] = part[:, my_tile]
        await_bytes(held.at[pl.ds(0, count - 1)], sems.at[0])

        def add(k, s):
            return s + held[k].astype(F32)

        return lax.fori_loop(0, count, add, jnp.zeros((slots, LANES), F32), unroll=4)

    @pl.when(me < tiles)
    def _():
        acc_parts[my_f] = col_acc_ref[:, my_tile]
        await_bytes(acc_parts.at[pl.ds(0, fsdp - 1)], sems.at[1])
        for f in range(fsdp):
            acc_all[f * own : (f + 1) * own, :] = acc_parts[f]
        new = DECAY_RATE * acc_all[...] + (1.0 - DECAY_RATE) * tile_sum() / size
        total[...] = new.astype(BF16)

    @pl.when(me == tiles)
    def _():
        s = tile_sum()
        both = jnp.where(
            wide_lane < STATS, s + pltpu.roll(s, LANES - STATS, 1), s + pltpu.roll(s, STATS, 1)
        )
        top = both.astype(BF16).astype(F32)
        total[...] = jnp.where(wide_lane < STATS, top, both - top).astype(BF16)

    def total_copy(k):
        to = lax.rem(me + k, count)
        return copy(total, cols.at[:, my_tile], 4, to // rep, lax.rem(to, rep))

    @pl.when(me < all_tiles)
    def _():
        def send(k, _):
            total_copy(k).start()
            return 0

        lax.fori_loop(1, count, send, 0)
        cols[:, my_tile] = total[...]

    await_bytes(hidden_parts.at[pl.ds(0, fsdp - 1)], sems.at[2])
    await_bytes(cell_parts.at[pl.ds(0, fsdp - 1)], sems.at[3])
    for f in range(fsdp):
        hidden_out[f * own : (f + 1) * own, :] = hidden_parts[f]
        cell_out[f * own : (f + 1) * own, :] = cell_parts[f]

    def await_tiles(number):
        await_bytes(cols.at[:, pl.ds(0, number * LANES)], sems.at[4])
        await_bytes(part.at[:, pl.ds(0, number * LANES)], send_sem.at[0])

    pl.when(me < all_tiles)(lambda: await_tiles(all_tiles - 1))
    pl.when(me >= all_tiles)(lambda: await_tiles(all_tiles))
    cols_out[...] = cols[...]

    for q in range(acc_steps):
        pl.when((q != my_f) & (q * rep + my_r < tiles))(lambda q=q: acc_copy(q).wait_send())
    await_bytes(hidden_parts.at[pl.ds(0, fsdp - 1)], send_sem.at[2])
    await_bytes(cell_parts.at[pl.ds(0, fsdp - 1)], send_sem.at[3])

    @pl.when(me < all_tiles)
    def _():
        await_bytes(held.at[pl.ds(0, count - 1)], send_sem.at[4])


def update_kernel(
    rep,
    own,
    params_ref,
    grads_ref,
    moments_ref,
    row_acc_ref,
    lengths_ref,
    order_ref,
    cols_ref,
    hidden_ref,
    cell_ref,
    rows_ref,
    lstm_in_ref,
    lstm_rec_ref,
    lstm_bias_ref,
    hyper_first_ref,
    hyper_rest_ref,
    update_ref,
    row_new_ref,
    col_new_ref,
    hidden_new_ref,
    cell_new_ref,
    cols_f32,
    w_first,
    w_second,
):
    my_f = lax.axis_index("fsdp")
    me = my_f * rep + lax.axis_index("rep")
    row_count, width = params_ref.shape
    slots, hid = hidden_ref.shape
    hm = hyper_rest_ref.shape[1] // 4
    fin = hyper_first_ref.shape[1] // hm
    outs = (hyper_rest_ref.shape[1] - hm) // hm
    mine = my_f * own

    lengths = lengths_ref[...].astype(F32)
    order = order_ref[...].astype(F32)
    start, size = slot_columns(lengths, order)

    cols_f32[...] = cols_ref[:, :width].astype(F32)
    take_rows(cols_f32[...], mine, col_new_ref)
    col_mean = jnp.mean(cols_f32[...], axis=1, keepdims=True)
    col_square = jnp.mean(cols_f32[...] * cols_f32[...], axis=1, keepdims=True)
    sent = cols_ref[:, width:].astype(F32)
    stats = (sent + pltpu.roll(sent, LANES - STATS, 1)) / (size * width)
    mean = [stats[:, k : k + 1] for k in range(STATS)]
    features = [jnp.log(mean[k] + EPSILON) for k in range(5)] + [
        mean[5] / jnp.sqrt(mean[0] * mean[1] + EPSILON),
        mean[6] / jnp.sqrt(mean[0] * mean[3] + EPSILON),
        mean[7] / jnp.sqrt(mean[1] * mean[3] + EPSILON),
        jnp.log(col_mean + EPSILON),
        jnp.log(col_square / (col_mean * col_mean)),
    ]
    ft = lstm_in_ref.shape[0]
    lane = iota((slots, ft), 1)
    feature_table = jnp.zeros((slots, ft), F32)
    for k, f in enumerate(features):
        feature_table = jnp.where(lane == k, f, feature_table)
    gates = (
        jnp.dot(feature_table.astype(BF16), lstm_in_ref[...], preferred_element_type=F32)
        + jnp.dot(hidden_ref[...].astype(BF16), lstm_rec_ref[...], preferred_element_type=F32)
        + lstm_bias_ref[...]
    )
    cell_new = jax.nn.sigmoid(gates[:, hid : 2 * hid]) * cell_ref[...] + jax.nn.sigmoid(
        gates[:, :hid]
    ) * jnp.tanh(gates[:, 2 * hid : 3 * hid])
    hidden_new = jax.nn.sigmoid(gates[:, 3 * hid :]) * jnp.tanh(cell_new)
    take_rows(hidden_new, mine, hidden_new_ref)
    take_rows(cell_new, mine, cell_new_ref)
    hidden_bf = hidden_new.astype(BF16)
    first_all = jnp.dot(hidden_bf, hyper_first_ref[...], preferred_element_type=F32).astype(BF16)
    rest_all = jnp.dot(hidden_bf, hyper_rest_ref[...], preferred_element_type=F32).astype(BF16)
    wide_lane = iota((slots, LANES), 1)
    scales = jnp.where(
        wide_lane == 0,
        lax.rsqrt(mean[0] + EPSILON),
        jnp.where(
            wide_lane == 1,
            lax.rsqrt(mean[1] + EPSILON),
            jnp.where(wide_lane == 2, lax.rsqrt(mean[4] + EPSILON), 1.0 / col_mean),
        ),
    )

    start_row, size_row = to_row(start), to_row(size)
    row_ids = (me * row_count + iota((row_count, slots), 0)).astype(F32)
    pick = jnp.where((row_ids >= start_row) & (row_ids < start_row + size_row), 1.0, 0.0)
    pick_bf = pick.astype(BF16)
    scale_rows = jnp.dot(
        pick, scales, precision=lax.Precision.HIGHEST, preferred_element_type=F32
    )
    row_new = DECAY_RATE * to_column(row_acc_ref[...]) + ((1.0 - DECAY_RATE) / width) * rows_ref[:, :1]
    row_new_ref[...] = to_row(row_new)
    row_coef = row_new * scale_rows[:, 3:4]

    fh = fin * hm
    swap = jnp.where(
        iota((fh, fh), 0) == lax.rem(iota((fh, fh), 1), fin) * hm + iota((fh, fh), 1) // fin, 1.0, 0.0
    ).astype(BF16)
    first_swapped = jnp.dot(first_all, swap, preferred_element_type=F32).astype(BF16)
    first_rows = jnp.dot(pick_bf, first_swapped, preferred_element_type=F32).astype(BF16)
    rest_rows = jnp.dot(pick_bf, rest_all, preferred_element_type=F32)
    rest_bf = rest_rows.astype(BF16)
    wide = fin * GROUP
    per = LANES // fin
    spread_shape = (LANES, per * wide)
    column = iota(spread_shape, 1)
    spread = jnp.where(
        iota(spread_shape, 0) == (column // wide) * fin + lax.rem(column, wide) // GROUP, 1.0, 0.0
    ).astype(BF16)
    first_wide = [
        jnp.dot(first_rows[:, j : j + LANES], spread, preferred_element_type=F32)
        for j in range(0, fh, LANES)
    ]
    on_diag = lax.rem(iota((GROUP, wide), 1), GROUP) == iota((GROUP, wide), 0)
    eye = iota((GROUP, GROUP), 0) == iota((GROUP, GROUP), 1)
    second_shape = (hyper_rest_ref.shape[1], hm * GROUP)
    on_second = lax.rem(iota((GROUP, hm * GROUP), 1), GROUP) == iota((GROUP, hm * GROUP), 0)
    groups = row_count // GROUP
    for h in range(hm):
        source = first_wide[h // per]
        at = (h % per) * wide
        for g in range(groups):
            rows = slice(g * GROUP, (g + 1) * GROUP)
            place = slice(h * GROUP, (h + 1) * GROUP)
            w_first[g, place, :wide] = jnp.where(
                on_diag, source[rows, at : at + wide], 0.0
            ).astype(BF16)
            w_first[g, place, wide:] = jnp.where(eye, rest_rows[rows, h : h + 1], 0.0).astype(BF16)
    for o in range(outs):
        pattern = jnp.where(
            iota(second_shape, 0) == hm + (iota(second_shape, 1) // GROUP) * outs + o, 1.0, 0.0
        ).astype(BF16)
        second = jnp.dot(rest_bf, pattern, preferred_element_type=F32)
        for g in range(groups):
            w_second[g, o * GROUP : (o + 1) * GROUP, :] = jnp.where(
                on_second, second[g * GROUP : (g + 1) * GROUP], 0.0
            ).astype(BF16)

    step = LANES * math.gcd(width // LANES, 2)
    ones = jnp.ones((GROUP, step), BF16)

    @pl.loop(0, width // step)
    def _(k):
        at = pl.ds(pl.multiple_of(k * step, LANES), step)
        col_rows = jnp.dot(pick_bf, cols_ref[:, at], preferred_element_type=F32)
        for g in range(groups):
            rows = slice(g * GROUP, (g + 1) * GROUP)
            inv = lax.rsqrt(col_rows[rows] * row_coef[rows] + EPSILON)
            grad = grads_ref[rows, at].astype(F32)
            mom = moments_ref[0, rows, at].astype(F32)
            grad_norm = grad * inv
            mom_norm = mom * inv
            parts = (
                grad_norm,
                mom_norm,
                moments_ref[1, rows, at].astype(F32) * inv,
                moments_ref[2, rows, at].astype(F32) * inv,
                grad * scale_rows[rows, 0:1],
                mom * scale_rows[rows, 1:2],
                params_ref[rows, at] * scale_rows[rows, 2:3],
                grad_norm * mom_norm,
            )
            inputs = jnp.concatenate([x.astype(BF16) for x in parts] + [ones], axis=0)
            units = jnp.dot(w_first[g], inputs, preferred_element_type=F32)
            units = jnp.maximum(units.astype(BF16), jnp.zeros((), BF16))
            result = jnp.dot(w_second[g], units, preferred_element_type=F32)
            update_ref[rows, at] = (
                result[:GROUP]
                * jnp.exp(jnp.tanh(result[GROUP : 2 * GROUP]))
                * jax.nn.sigmoid(result[2 * GROUP :])
            )


def on_device(
    fsdp,
    rep,
    params,
    grads,
    moments,
    row_acc,
    lengths,
    tensor_order,
    col_acc,
    hidden_state,
    cell_state,
    lstm_in,
    lstm_rec,
    lstm_bias,
    hyper_first,
    hyper_rest,
):
    count = fsdp * rep
    row_count, width = params.shape
    slots = lengths.shape[0]
    own, hid = hidden_state.shape
    hm = hyper_rest.shape[1] // 4
    fin = hyper_first.shape[1] // hm
    outs = (hyper_rest.shape[1] - hm) // hm
    groups = row_count // GROUP
    lengths = lengths.reshape(1, slots)
    order = tensor_order.reshape(1, slots)
    in_vmem = pl.BlockSpec(memory_space=pltpu.VMEM)

    cols, hidden_all, cell_all, row_stats = pl.pallas_call(
        functools.partial(share_kernel, fsdp, rep),
        out_shape=(
            jax.ShapeDtypeStruct((slots, width + LANES), BF16),
            jax.ShapeDtypeStruct((slots, hid), F32),
            jax.ShapeDtypeStruct((slots, hid), F32),
            jax.ShapeDtypeStruct((row_count, LANES), F32),
        ),
        in_specs=[in_vmem] * 8,
        out_specs=[in_vmem] * 4,
        scratch_shapes=[
            pltpu.VMEM((slots, width + LANES), BF16),
            pltpu.VMEM((count, slots, LANES), BF16),
            pltpu.VMEM((slots, LANES), BF16),
            pltpu.VMEM((slots, width + LANES), BF16),
            pltpu.VMEM((fsdp, own, LANES), F32),
            pltpu.VMEM((slots, LANES), F32),
            pltpu.VMEM((fsdp, own, hid), F32),
            pltpu.VMEM((fsdp, own, hid), F32),
            pltpu.SemaphoreType.DMA((5,)),
            pltpu.SemaphoreType.DMA((5,)),
            pltpu.SemaphoreType.DMA((-(-(width // LANES) // rep),)),
        ],
        compiler_params=pltpu.CompilerParams(collective_id=0, has_side_effects=True),
        name="share",
    )(params, grads, moments, lengths, order, col_acc, hidden_state, cell_state)

    update, row_new, col_new, hidden_new, cell_new = pl.pallas_call(
        functools.partial(update_kernel, rep, own),
        out_shape=(
            jax.ShapeDtypeStruct((row_count, width), F32),
            jax.ShapeDtypeStruct((1, row_count), F32),
            jax.ShapeDtypeStruct((own, width), F32),
            jax.ShapeDtypeStruct((own, hid), F32),
            jax.ShapeDtypeStruct((own, hid), F32),
        ),
        in_specs=[in_vmem] * 15,
        out_specs=[in_vmem] * 5,
        scratch_shapes=[
            pltpu.VMEM((slots, width), F32),
            pltpu.VMEM((groups, hm * GROUP, (fin + 1) * GROUP), BF16),
            pltpu.VMEM((groups, outs * GROUP, hm * GROUP), BF16),
        ],
        name="update",
    )(
        params,
        grads,
        moments,
        row_acc.reshape(1, row_count),
        lengths,
        order,
        cols,
        hidden_all,
        cell_all,
        row_stats,
        lstm_in,
        lstm_rec,
        lstm_bias.reshape(1, -1),
        hyper_first,
        hyper_rest,
    )
    return (update, row_new.reshape(row_count), col_new, hidden_new, cell_new)


def solution(mesh):
    rows = P(("fsdp", "rep"), None)
    flat = P(("fsdp", "rep"))
    own = P("fsdp", None)
    return jax.shard_map(
        functools.partial(on_device, mesh.shape["fsdp"], mesh.shape["rep"]),
        mesh=mesh,
        in_specs=(rows, rows, P(None, ("fsdp", "rep"), None), flat, P(), P(), own, own, own)
        + (P(),) * 5,
        out_specs=(rows, flat, own, own, own),
        check_vma=False,
    )
```

time: 247 us -> 45 us (0.18)
  the two profiles are of different devices: /device:TPU:0 before, /device:TPU:25 now
where the time goes in v1:
time: 45 us; the launch traced here: 44.9 us
  Pallas kernels  44.2 us (98%)
  between operations  0.64 us (1%)
    pallas_call x1, Pallas kernels, on_device(): pl.pallas_call(functools.partial(share_kernel, fsdp, rep), out_shape=(jax...  24.5 us
    pallas_call x1, Pallas kernels, on_device(): pl.pallas_call(functools.partial(update_kernel, rep, own), out_shape=(jax...  19.7 us

profile of v1, /device:TPU:25, one launch (start us, length us, event | category | flops | bytes accessed | tf_op | source)
XLA Modules:
  0.0 44.9 jit_solution(3598305467030648194)
XLA Ops:
  0.6 24.5 %share.1 = (bf16[32,3712]{1,0:T(8,128)(2,1)}, f32[32,512]{1,0:T(8,128)}, f32[32,512]{1,0:T(8,128)}, f32[48,128]{1,0:T(8,128)}) custom-call(f32[48,3584]{1,0:T(8,128)} %params_ref.3, bf16[48,3584]{1,0:T(8,128)(2,1)} %grads_ref.3, bf16[3,48,3584]{2,1,0:T(8,128)(2,1)} %moments_ref.3, s32[1,32]{1,0:T(1,128)} %bitcast.6, s32[1,32]{1,0:T(1,128)} %bitcast.8, ...), custom_call_target="tpu_custom_call" | custom-call | tf_op jit(solution)/shard_map/share/pallas_call | solution.py:465
  25.1 19.7 %update.1 = (f32[48,3584]{1,0:T(8,128)}, f32[1,48]{1,0:T(1,128)}, f32[2,3584]{1,0:T(2,128)}, f32[2,512]{1,0:T(2,128)}, f32[2,512]{1,0:T(2,128)}) custom-call(f32[48,3584]{1,0:T(8,128)} %params_ref.3, bf16[48,3584]{1,0:T(8,128)(2,1)} %grads_ref.3, bf16[3,48,3584]{2,1,0:T(8,128)(2,1)} %moments_ref.3, f32[1,48]{1,0:T(1,128)} %bitcast.10, s32[1,32]{1,0:T(1,128)} %bitcast.7, ...), custom_call_target="tpu_custom_call" | custom-call | tf_op jit(solution)/shard_map/update/pallas_call | solution.py:492

commit v2 on v1

--- a/solution.py
+++ b/solution.py
@@ -49,32 +49,51 @@
     return start, size
 
 
+def split_stats(sums, lane):
+    both = jnp.where(
+        lane < STATS, sums + pltpu.roll(sums, LANES - STATS, 1), sums + pltpu.roll(sums, STATS, 1)
+    )
+    top = both.astype(BF16).astype(F32)
+    return jnp.where(lane < STATS, top, both - top).astype(BF16)
+
+
 def share_kernel(
     fsdp,
     rep,
-    params_ref,
-    grads_ref,
-    moments_ref,
+    params_hbm,
+    grads_hbm,
+    moments_hbm,
+    rec_hbm,
+    bias_ref,
     lengths_ref,
     order_ref,
     col_acc_ref,
     hidden_ref,
     cell_ref,
     cols_out,
-    hidden_out,
+    gates_out,
     cell_out,
     rows_out,
+    params_ref,
+    grads_ref,
+    moments_ref,
+    rec_ref,
     part,
+    pair,
+    mid,
     held,
     total,
     cols,
     acc_parts,
     acc_all,
     hidden_parts,
+    hidden_all,
     cell_parts,
-    sems,
+    load_sem,
+    recv_sem,
     send_sem,
     acc_sem,
+    mid_sem,
 ):
     count = fsdp * rep
     my_f = lax.axis_index("fsdp")
@@ -84,7 +103,8 @@
     slots = lengths_ref.shape[1]
     own = slots // fsdp
     tiles = width // LANES
-    all_tiles = tiles + 1
+    per_rep = -(-(tiles + 1) // rep)
+    block = per_rep * LANES
     barrier = pltpu.get_barrier_semaphore()
 
     def hello(k, _):
@@ -98,12 +118,68 @@
         return 0
 
     lax.fori_loop(1, count, hello, 0)
+    loads = [
+        pltpu.make_async_copy(src, dst, load_sem.at[k])
+        for k, (src, dst) in enumerate(
+            (
+                (grads_hbm, grads_ref),
+                (moments_hbm, moments_ref),
+                (params_hbm, params_ref),
+                (rec_hbm, rec_ref),
+            )
+        )
+    ]
+    for c in loads:
+        c.start()
+
+    def await_bytes(ref, sem):
+        pltpu.make_async_copy(ref, ref, sem).wait()
+
+    def copy(src, dst, which, to_f, to_r, sending=None):
+        return pltpu.make_async_remote_copy(
+            src_ref=src,
+            dst_ref=dst,
+            send_sem=send_sem.at[which] if sending is None else sending,
+            recv_sem=recv_sem.at[which],
+            device_id=(to_f, to_r),
+            device_id_type=pl.DeviceIdType.MESH,
+        )
 
     start, size = slot_columns(lengths_ref[...].astype(F32), order_ref[...].astype(F32))
     row_ids = (me * row_count + iota((slots, row_count), 1)).astype(F32)
     pick = jnp.where((row_ids >= start) & (row_ids < start + size), 1.0, 0.0)
 
+    pl.semaphore_wait(barrier, count - 1)
+
+    def state_copies(k):
+        to = lax.rem(my_f + k, fsdp)
+        return (
+            copy(hidden_ref, hidden_parts.at[my_f], 2, to, my_r),
+            copy(cell_ref, cell_parts.at[my_f], 3, to, my_r),
+        )
+
+    def acc_copy(q):
+        tile = jnp.minimum(my_r * per_rep + q, tiles - 1)
+        at = pl.ds(pl.multiple_of(tile * LANES, LANES), LANES)
+        return copy(col_acc_ref.at[:, at], acc_parts.at[my_f], 1, q, my_r, acc_sem.at[q])
+
+    def sends_acc(q):
+        return (q != my_f) & (my_r * per_rep + q < tiles)
+
+    def send_states(k, _):
+        for c in state_copies(k):
+            c.start()
+        return 0
+
+    for q in range(per_rep):
+        pl.when(sends_acc(q))(lambda q=q: acc_copy(q).start())
+    lax.fori_loop(1, fsdp, send_states, 0)
+    hidden_parts[my_f] = hidden_ref[...]
+    cell_parts[my_f] = cell_ref[...]
+
     step = LANES * math.gcd(tiles, 4)
+    for c in loads[:3]:
+        c.wait()
     lane = iota((GROUP, LANES), 1)
     for first in range(0, row_count, GROUP):
         rows = pl.ds(first, GROUP)
@@ -136,7 +212,9 @@
     )
     wide_lane = iota((slots, LANES), 1)
     high = slot_stats.astype(BF16).astype(F32)
-    part[:, width:] = jnp.where(wide_lane < STATS, high, slot_stats - high).astype(BF16)
+    part[:, width : width + LANES] = jnp.where(wide_lane < STATS, high, slot_stats - high).astype(BF16)
+    if rep * per_rep > tiles + 1:
+        part[:, width + LANES :] = jnp.zeros((slots, rep * block - width - LANES), BF16)
     pick_bf = pick.astype(BF16)
     for first in range(0, width, step):
         g = grads_ref[:, first : first + step].astype(F32)
@@ -144,118 +222,114 @@
             pick_bf, (g * g).astype(BF16), preferred_element_type=F32
         ).astype(BF16)
 
-    pl.semaphore_wait(barrier, count - 1)
-
-    def await_bytes(ref, sem):
-        pltpu.make_async_copy(ref, ref, sem).wait()
-
-    def copy(src, dst, which, to_f, to_r, sending=None):
-        return pltpu.make_async_remote_copy(
-            src_ref=src,
-            dst_ref=dst,
-            send_sem=send_sem.at[which] if sending is None else sending,
-            recv_sem=sems.at[which],
-            device_id=(to_f, to_r),
-            device_id_type=pl.DeviceIdType.MESH,
+    def block_of(r):
+        return pl.ds(pl.multiple_of(r * block, LANES), block)
+
+    def pair_copy(k):
+        to = lax.rem(my_r + k, rep)
+        return copy(part.at[:, block_of(to)], pair.at[my_r], 0, my_f, to)
+
+    for k in range(1, rep):
+        pair_copy(k).start()
+    pair[my_r] = part[:, block_of(my_r)]
+    await_bytes(pair.at[pl.ds(0, rep - 1)], recv_sem.at[0])
+    stats_rep, stats_at = tiles // per_rep, tiles % per_rep
+    for q in range(per_rep):
+        at = slice(q * LANES, (q + 1) * LANES)
+        s = pair[0, :, at].astype(F32)
+        for r in range(1, rep):
+            s = s + pair[r, :, at].astype(F32)
+        value = s.astype(BF16)
+        if q == stats_at:
+            value = jnp.where(my_r == stats_rep, split_stats(s, wide_lane), value)
+        mid[:, at] = value
+
+    def mid_copy(q):
+        return copy(
+            mid.at[:, pl.ds(q * LANES, LANES)], held.at[my_f], 5, q, my_r, mid_sem.at[q]
         )
 
-    my_tile = pl.ds(pl.multiple_of(jnp.minimum(me, all_tiles - 1) * LANES, LANES), LANES)
-
-    def part_copy(tile):
-        return copy(
-            part.at[:, pl.ds(tile * LANES, LANES)], held.at[me], 0, tile // rep, tile % rep
-        )
-
-    for tile in range(all_tiles):
-        pl.when(me != tile)(lambda tile=tile: part_copy(tile).start())
-
-    def acc_copy(q):
-        tile = q * rep + my_r
-        at = pl.ds(pl.multiple_of(tile * LANES, LANES), LANES)
-        return copy(col_acc_ref.at[:, at], acc_parts.at[my_f], 1, q, my_r, acc_sem.at[q])
-
-    acc_steps = -(-tiles // rep)
-    for q in range(acc_steps):
-        pl.when((q != my_f) & (q * rep + my_r < tiles))(lambda q=q: acc_copy(q).start())
-
-    def state_copies(k):
-        to = lax.rem(my_f + k, fsdp)
-        return (
-            copy(hidden_ref, hidden_parts.at[my_f], 2, to, my_r),
-            copy(cell_ref, cell_parts.at[my_f], 3, to, my_r),
-        )
-
-    def send_states(k, _):
-        for c in state_copies(k):
-            c.start()
-        return 0
-
-    lax.fori_loop(1, fsdp, send_states, 0)
-    hidden_parts[my_f] = hidden_ref[...]
-    cell_parts[my_f] = cell_ref[...]
+    for q in range(per_rep):
+        pl.when(q != my_f)(lambda q=q: mid_copy(q).start())
+
+    await_bytes(hidden_parts.at[pl.ds(0, fsdp - 1)], recv_sem.at[2])
+    await_bytes(cell_parts.at[pl.ds(0, fsdp - 1)], recv_sem.at[3])
+    for f in range(fsdp):
+        hidden_all[f * own : (f + 1) * own, :] = hidden_parts[f]
+        cell_out[f * own : (f + 1) * own, :] = cell_parts[f]
+    loads[3].wait()
+    gates_out[...] = (
+        jnp.dot(hidden_all[...].astype(BF16), rec_ref[...], preferred_element_type=F32)
+        + bias_ref[...]
+    )
+
+    holds = my_f < per_rep
+    my_tile = my_r * per_rep + my_f
+    at_tile = pl.ds(
+        pl.multiple_of(jnp.minimum(my_tile, rep * per_rep - 1) * LANES, LANES), LANES
+    )
+    at_acc = pl.ds(pl.multiple_of(jnp.minimum(my_tile, tiles - 1) * LANES, LANES), LANES)
+    at_mid = pl.ds(pl.multiple_of(jnp.minimum(my_f, per_rep - 1) * LANES, LANES), LANES)
 
     def tile_sum():
-        held[me] = part[:, my_tile]
-        await_bytes(held.at[pl.ds(0, count - 1)], sems.at[0])
-
-        def add(k, s):
-            return s + held[k].astype(F32)
-
-        return lax.fori_loop(0, count, add, jnp.zeros((slots, LANES), F32), unroll=4)
-
-    @pl.when(me < tiles)
+        held[my_f] = mid[:, at_mid]
+        await_bytes(held.at[pl.ds(0, fsdp - 1)], recv_sem.at[5])
+        s = held[0].astype(F32)
+        for f in range(1, fsdp):
+            s = s + held[f].astype(F32)
+        return s
+
+    @pl.when(holds & (my_tile < tiles))
     def _():
-        acc_parts[my_f] = col_acc_ref[:, my_tile]
-        await_bytes(acc_parts.at[pl.ds(0, fsdp - 1)], sems.at[1])
+        acc_parts[my_f] = col_acc_ref[:, at_acc]
+        await_bytes(acc_parts.at[pl.ds(0, fsdp - 1)], recv_sem.at[1])
         for f in range(fsdp):
             acc_all[f * own : (f + 1) * own, :] = acc_parts[f]
         new = DECAY_RATE * acc_all[...] + (1.0 - DECAY_RATE) * tile_sum() / size
         total[...] = new.astype(BF16)
 
-    @pl.when(me == tiles)
+    @pl.when(holds & (my_tile >= tiles))
     def _():
-        s = tile_sum()
-        both = jnp.where(
-            wide_lane < STATS, s + pltpu.roll(s, LANES - STATS, 1), s + pltpu.roll(s, STATS, 1)
-        )
-        top = both.astype(BF16).astype(F32)
-        total[...] = jnp.where(wide_lane < STATS, top, both - top).astype(BF16)
+        total[...] = split_stats(tile_sum(), wide_lane)
 
     def total_copy(k):
-        to = lax.rem(me + k, count)
-        return copy(total, cols.at[:, my_tile], 4, to // rep, lax.rem(to, rep))
-
-    @pl.when(me < all_tiles)
+        return copy(total, cols.at[:, at_tile], 4, lax.rem(my_f + k, fsdp), my_r)
+
+    @pl.when(holds)
     def _():
         def send(k, _):
             total_copy(k).start()
             return 0
 
-        lax.fori_loop(1, count, send, 0)
-        cols[:, my_tile] = total[...]
-
-    await_bytes(hidden_parts.at[pl.ds(0, fsdp - 1)], sems.at[2])
-    await_bytes(cell_parts.at[pl.ds(0, fsdp - 1)], sems.at[3])
-    for f in range(fsdp):
-        hidden_out[f * own : (f + 1) * own, :] = hidden_parts[f]
-        cell_out[f * own : (f + 1) * own, :] = cell_parts[f]
+        lax.fori_loop(1, fsdp, send, 0)
+        cols[:, at_tile] = total[...]
 
     def await_tiles(number):
-        await_bytes(cols.at[:, pl.ds(0, number * LANES)], sems.at[4])
-        await_bytes(part.at[:, pl.ds(0, number * LANES)], send_sem.at[0])
-
-    pl.when(me < all_tiles)(lambda: await_tiles(all_tiles - 1))
-    pl.when(me >= all_tiles)(lambda: await_tiles(all_tiles))
+        await_bytes(cols.at[:, pl.ds(0, number * LANES)], recv_sem.at[4])
+
+    pl.when(holds)(lambda: await_tiles(per_rep - 1))
+    pl.when(jnp.logical_not(holds))(lambda: await_tiles(per_rep))
+
+    def block_copy(k):
+        here = cols.at[:, block_of(my_r)]
+        return copy(here, here, 6, my_f, lax.rem(my_r + k, rep))
+
+    for k in range(1, rep):
+        block_copy(k).start()
+    await_bytes(cols.at[:, pl.ds(0, (rep - 1) * block)], recv_sem.at[6])
     cols_out[...] = cols[...]
 
-    for q in range(acc_steps):
-        pl.when((q != my_f) & (q * rep + my_r < tiles))(lambda q=q: acc_copy(q).wait_send())
+    await_bytes(pair.at[pl.ds(0, rep - 1)], send_sem.at[0])
+    for q in range(per_rep):
+        pl.when(sends_acc(q))(lambda q=q: acc_copy(q).wait_send())
+        pl.when(q != my_f)(lambda q=q: mid_copy(q).wait_send())
     await_bytes(hidden_parts.at[pl.ds(0, fsdp - 1)], send_sem.at[2])
     await_bytes(cell_parts.at[pl.ds(0, fsdp - 1)], send_sem.at[3])
-
-    @pl.when(me < all_tiles)
+    await_bytes(cols.at[:, pl.ds(0, (rep - 1) * block)], send_sem.at[6])
+
+    @pl.when(holds)
     def _():
-        await_bytes(held.at[pl.ds(0, count - 1)], send_sem.at[4])
+        await_bytes(held.at[pl.ds(0, fsdp - 1)], send_sem.at[4])
 
 
 def update_kernel(
@@ -268,12 +342,10 @@
     lengths_ref,
     order_ref,
     cols_ref,
-    hidden_ref,
+    gates_ref,
     cell_ref,
     rows_ref,
     lstm_in_ref,
-    lstm_rec_ref,
-    lstm_bias_ref,
     hyper_first_ref,
     hyper_rest_ref,
     update_ref,
@@ -284,11 +356,12 @@
     cols_f32,
     w_first,
     w_second,
+    bias,
 ):
     my_f = lax.axis_index("fsdp")
     me = my_f * rep + lax.axis_index("rep")
     row_count, width = params_ref.shape
-    slots, hid = hidden_ref.shape
+    slots, hid = cell_ref.shape
     hm = hyper_rest_ref.shape[1] // 4
     fin = hyper_first_ref.shape[1] // hm
     outs = (hyper_rest_ref.shape[1] - hm) // hm
@@ -302,7 +375,7 @@
     take_rows(cols_f32[...], mine, col_new_ref)
     col_mean = jnp.mean(cols_f32[...], axis=1, keepdims=True)
     col_square = jnp.mean(cols_f32[...] * cols_f32[...], axis=1, keepdims=True)
-    sent = cols_ref[:, width:].astype(F32)
+    sent = cols_ref[:, width : width + LANES].astype(F32)
     stats = (sent + pltpu.roll(sent, LANES - STATS, 1)) / (size * width)
     mean = [stats[:, k : k + 1] for k in range(STATS)]
     features = [jnp.log(mean[k] + EPSILON) for k in range(5)] + [
@@ -317,10 +390,8 @@
     feature_table = jnp.zeros((slots, ft), F32)
     for k, f in enumerate(features):
         feature_table = jnp.where(lane == k, f, feature_table)
-    gates = (
-        jnp.dot(feature_table.astype(BF16), lstm_in_ref[...], preferred_element_type=F32)
-        + jnp.dot(hidden_ref[...].astype(BF16), lstm_rec_ref[...], preferred_element_type=F32)
-        + lstm_bias_ref[...]
+    gates = gates_ref[...] + jnp.dot(
+        feature_table.astype(BF16), lstm_in_ref[...], preferred_element_type=F32
     )
     cell_new = jax.nn.sigmoid(gates[:, hid : 2 * hid]) * cell_ref[...] + jax.nn.sigmoid(
         gates[:, :hid]
@@ -386,7 +457,7 @@
             w_first[g, place, :wide] = jnp.where(
                 on_diag, source[rows, at : at + wide], 0.0
             ).astype(BF16)
-            w_first[g, place, wide:] = jnp.where(eye, rest_rows[rows, h : h + 1], 0.0).astype(BF16)
+            bias[g, place, :] = jnp.broadcast_to(rest_bf[rows, h : h + 1].astype(F32), (GROUP, LANES))
     for o in range(outs):
         pattern = jnp.where(
             iota(second_shape, 0) == hm + (iota(second_shape, 1) // GROUP) * outs + o, 1.0, 0.0
@@ -397,8 +468,7 @@
                 on_second, second[g * GROUP : (g + 1) * GROUP], 0.0
             ).astype(BF16)
 
-    step = LANES * math.gcd(width // LANES, 2)
-    ones = jnp.ones((GROUP, step), BF16)
+    step = LANES * math.gcd(width // LANES, 14)
 
     @pl.loop(0, width // step)
     def _(k):
@@ -421,8 +491,9 @@
                 params_ref[rows, at] * scale_rows[rows, 2:3],
                 grad_norm * mom_norm,
             )
-            inputs = jnp.concatenate([x.astype(BF16) for x in parts] + [ones], axis=0)
+            inputs = jnp.concatenate([x.astype(BF16) for x in parts], axis=0)
             units = jnp.dot(w_first[g], inputs, preferred_element_type=F32)
+            units = units + jnp.concatenate([bias[g]] * (step // LANES), axis=1)
             units = jnp.maximum(units.astype(BF16), jnp.zeros((), BF16))
             result = jnp.dot(w_second[g], units, preferred_element_type=F32)
             update_ref[rows, at] = (
@@ -450,7 +521,6 @@
     hyper_first,
     hyper_rest,
 ):
-    count = fsdp * rep
     row_count, width = params.shape
     slots = lengths.shape[0]
     own, hid = hidden_state.shape
@@ -462,32 +532,56 @@
     order = tensor_order.reshape(1, slots)
     in_vmem = pl.BlockSpec(memory_space=pltpu.VMEM)
 
-    cols, hidden_all, cell_all, row_stats = pl.pallas_call(
+    anywhere = pl.BlockSpec(memory_space=pl.ANY)
+    per_rep = -(-(width // LANES + 1) // rep)
+    padded = rep * per_rep * LANES
+
+    cols, gates, cell_all, row_stats = pl.pallas_call(
         functools.partial(share_kernel, fsdp, rep),
         out_shape=(
-            jax.ShapeDtypeStruct((slots, width + LANES), BF16),
-            jax.ShapeDtypeStruct((slots, hid), F32),
+            jax.ShapeDtypeStruct((slots, padded), BF16),
+            jax.ShapeDtypeStruct((slots, lstm_rec.shape[1]), F32),
             jax.ShapeDtypeStruct((slots, hid), F32),
             jax.ShapeDtypeStruct((row_count, LANES), F32),
         ),
-        in_specs=[in_vmem] * 8,
+        in_specs=[anywhere] * 4 + [in_vmem] * 6,
         out_specs=[in_vmem] * 4,
         scratch_shapes=[
-            pltpu.VMEM((slots, width + LANES), BF16),
-            pltpu.VMEM((count, slots, LANES), BF16),
+            pltpu.VMEM(params.shape, params.dtype),
+            pltpu.VMEM(grads.shape, grads.dtype),
+            pltpu.VMEM(moments.shape, moments.dtype),
+            pltpu.VMEM(lstm_rec.shape, lstm_rec.dtype),
+            pltpu.VMEM((slots, padded), BF16),
+            pltpu.VMEM((rep, slots, per_rep * LANES), BF16),
+            pltpu.VMEM((slots, per_rep * LANES), BF16),
+            pltpu.VMEM((fsdp, slots, LANES), BF16),
             pltpu.VMEM((slots, LANES), BF16),
-            pltpu.VMEM((slots, width + LANES), BF16),
+            pltpu.VMEM((slots, padded), BF16),
             pltpu.VMEM((fsdp, own, LANES), F32),
             pltpu.VMEM((slots, LANES), F32),
             pltpu.VMEM((fsdp, own, hid), F32),
+            pltpu.VMEM((slots, hid), F32),
             pltpu.VMEM((fsdp, own, hid), F32),
-            pltpu.SemaphoreType.DMA((5,)),
-            pltpu.SemaphoreType.DMA((5,)),
-            pltpu.SemaphoreType.DMA((-(-(width // LANES) // rep),)),
+            pltpu.SemaphoreType.DMA((4,)),
+            pltpu.SemaphoreType.DMA((7,)),
+            pltpu.SemaphoreType.DMA((7,)),
+            pltpu.SemaphoreType.DMA((per_rep,)),
+            pltpu.SemaphoreType.DMA((per_rep,)),
         ],
         compiler_params=pltpu.CompilerParams(collective_id=0, has_side_effects=True),
         name="share",
-    )(params, grads, moments, lengths, order, col_acc, hidden_state, cell_state)
+    )(
+        params,
+        grads,
+        moments,
+        lstm_rec,
+        lstm_bias.reshape(1, -1),
+        lengths,
+        order,
+        col_acc,
+        hidden_state,
+        cell_state,
+    )
 
     update, row_new, col_new, hidden_new, cell_new = pl.pallas_call(
         functools.partial(update_kernel, rep, own),
@@ -498,12 +592,13 @@
             jax.ShapeDtypeStruct((own, hid), F32),
             jax.ShapeDtypeStruct((own, hid), F32),
         ),
-        in_specs=[in_vmem] * 15,
+        in_specs=[in_vmem] * 13,
         out_specs=[in_vmem] * 5,
         scratch_shapes=[
             pltpu.VMEM((slots, width), F32),
-            pltpu.VMEM((groups, hm * GROUP, (fin + 1) * GROUP), BF16),
+            pltpu.VMEM((groups, hm * GROUP, fin * GROUP), BF16),
             pltpu.VMEM((groups, outs * GROUP, hm * GROUP), BF16),
+            pltpu.VMEM((groups, hm * GROUP, LANES), F32),
         ],
         name="update",
     )(
@@ -514,12 +609,10 @@
         lengths,
         order,
         cols,
-        hidden_all,
+        gates,
         cell_all,
         row_stats,
         lstm_in,
-        lstm_rec,
-        lstm_bias.reshape(1, -1),
         hyper_first,
         hyper_rest,
     )

time: 45 us -> 32.6 us (0.72)
  the two profiles are of different devices: /device:TPU:25 before, /device:TPU:0 now
where the time goes in v2:
time: 32.6 us; the launch traced here: 32.3 us
  Pallas kernels  31.7 us (97%)
  between operations  0.64 us (2%)
    pallas_call x1, Pallas kernels, on_device(): pl.pallas_call(functools.partial(share_kernel, fsdp, rep), out_shape=(jax...  22.4 us
    pallas_call x1, Pallas kernels, on_device(): pl.pallas_call(functools.partial(update_kernel, rep, own), out_shape=(jax...  9.3 us

profile of v2, /device:TPU:0, one launch (start us, length us, event | category | flops | bytes accessed | tf_op | source)
XLA Modules:
  0.0 32.3 jit_solution(15447583875294488319)
XLA Ops:
  0.6 22.4 %share.1 = (bf16[32,3840]{1,0:T(8,128)(2,1)}, f32[32,2048]{1,0:T(8,128)}, f32[32,512]{1,0:T(8,128)}, f32[48,128]{1,0:T(8,128)}) custom-call(f32[48,3584]{1,0:T(8,128)} %params_ref.1, bf16[48,3584]{1,0:T(8,128)(2,1)} %grads_ref.1, bf16[3,48,3584]{2,1,0:T(8,128)(2,1)} %moments_ref.1, bf16[512,2048]{1,0:T(8,128)(2,1)} %rec_hbm.1, f32[1,2048]{1,0:T(1,128)} %bitcast.5, ...), custom_call_target="tpu_custom_call" | custom-call | tf_op jit(solution)/shard_map/share/pallas_call | solution.py:539
  23.0 9.3 %update.1 = (f32[48,3584]{1,0:T(8,128)}, f32[1,48]{1,0:T(1,128)}, f32[2,3584]{1,0:T(2,128)}, f32[2,512]{1,0:T(2,128)}, f32[2,512]{1,0:T(2,128)}) custom-call(f32[48,3584]{1,0:T(8,128)} %params_ref.1, bf16[48,3584]{1,0:T(8,128)(2,1)} %grads_ref.1, bf16[3,48,3584]{2,1,0:T(8,128)(2,1)} %moments_ref.1, f32[1,48]{1,0:T(1,128)} %bitcast.10, s32[1,32]{1,0:T(1,128)} %bitcast.7, ...), custom_call_target="tpu_custom_call" | custom-call | tf_op jit(solution)/shard_map/update/pallas_call | solution.py:586
